TPU v7x, 32 devices: a whole 2x2x4 slice. The times are simulated.
32 devices in a mesh: row: 4 (over y, x), col: 8 (over z, core).
Axes of the slice: x: 2, y: 2, z: 4, core: 2. Of those that a mesh axis runs over, the one named last changes fastest.
Arguments:
- amplitudes: bfloat16 [800, 800, 768], P('row', 'col'), may hold values from -6 to 6
- integrals: bfloat16 [800, 800, 256], P('row', 'col'), may hold values from -0.375 to 0.375
- window_index: int32 [256], replicated, may hold values from 0 to 639999, as said below
Outputs:
- residual: bfloat16 [800, 800, 768], P('row', 'col')
- pair_energy: float32 [768], replicated
Inputs may be any that keep to these rules, and one draw needn't show every extreme that they name: `window_index`: the window pairs are distinct; pair k lies in the block of a rows and b columns owned by device number k // 8 in row-major order of the (a, b) device grid, 8 pairs for each block.
All inputs are finite; a program needn't handle non-finite values.
Results may differ from a plain program's by a relative error of at most 0.001.
Values may be sent and summed in bfloat16 or wider, within the bound.
A program may use at most 256 MiB of HBM per device.

v0:
```python
import jax
import jax.numpy as jnp
from jax import lax
from jax.sharding import PartitionSpec as P


def shards(amplitudes, integrals, window_index):
    block_rows, block_cols, pairs = amplitudes.shape
    window = integrals.shape[2]
    ncols = lax.axis_size("col")
    nrows = lax.axis_size("row")
    per_device = window // (nrows * ncols)
    row_rank = lax.axis_index("row")
    col_rank = lax.axis_index("col")
    linear_rank = row_rank * ncols + col_rank
    owned_index = lax.dynamic_slice_in_dim(window_index, linear_rank * per_device, per_device)
    virtuals = block_rows * nrows
    row_offset = owned_index // virtuals - row_rank * block_rows
    col_offset = owned_index % virtuals - col_rank * block_cols
    owned = amplitudes[row_offset, col_offset]
    in_row = lax.all_gather(owned, "col", axis=0, tiled=True)
    columns = lax.all_gather(in_row, "row", axis=0, tiled=True)
    full = jnp.einsum("abk,kp->abp", integrals, columns, preferred_element_type=jnp.float32)
    partial_value = jnp.sum(amplitudes.astype(jnp.float32) * full, axis=(0, 1))
    pair_energy = lax.psum(partial_value, ("row", "col")) / virtuals
    residual = full.astype(jnp.bfloat16)
    return (residual, pair_energy)


def solution(mesh):
    return jax.shard_map(
        shards,
        mesh=mesh,
        in_specs=(P("row", "col", None), P("row", "col", None), P()),
        out_specs=(P("row", "col", None), P()),
        check_vma=False,
    )
```

profile of v0, /device:TPU:0, one launch (start us, length us, event | category | flops | bytes accessed | tf_op | source)
XLA Modules:
  0.0 172.8 jit_solution(1093921430304254708)
XLA Ops:
  0.6 0.8 fusion.7
  1.4 1.4 gather_fusion
  2.8 15.6 %all_gather.6 = bf16[64,768]{1,0:T(8,128)(2,1)S(1)} all-gather(bf16[8,768]{1,0:T(8,128)(2,1)S(1)} %gather_fusion), channel_id=1, replica_groups=mesh['row'=4,'col'=8] {'col'}, dimensions={0}, use_global_device_ids=true | all-gather | bytes 110592 | tf_op jit(solution)/shard_map/all_gather | solution.py:21
  18.4 9.5 %all_gather.7 = bf16[256,768]{1,0:T(8,128)(2,1)S(1)} all-gather(bf16[64,768]{1,0:T(8,128)(2,1)S(1)} %all_gather.6), channel_id=1, replica_groups=mesh['row'=4,'col'=8] {'row'}, dimensions={0}, use_global_device_ids=true | all-gather | bytes 491520 | tf_op jit(solution)/shard_map/all_gather | solution.py:22
  27.9 44.0 %bitcast_convert_fusion = (bf16[200,100,768]{2,1,0:T(8,128)(2,1)}, f32[768,200,100]{0,2,1:T(8,128)}) fusion(bf16[200,100,256]{2,0,1:T(8,128)(2,1)} %param.4, bf16[256,768]{1,0:T(8,128)(2,1)S(1)} %all_gather.7), kind=kOutput, calls=%fused_computation.2 | convolution fusion | flops 7879680000 | bytes 102793216 | tf_op jit(solution)/shard_map/abk,kp->abp/dot_general | solution.py:23
  71.9 22.0 %copy.7 = bf16[200,100,768]{2,0,1:T(8,128)(2,1)} copy(bf16[200,100,768]{2,1,0:T(8,128)(2,1)} %get-tuple-element.4) | data formatting | bytes 61440000
  93.9 39.0 %fusion = f32[768]{0:T(1024)S(1)} fusion(f32[768,200,100]{0,2,1:T(8,128)} %get-tuple-element.5, bf16[200,100,768]{2,0,1:T(8,128)(2,1)} %param.3), kind=kLoop, calls=%fused_computation.3 | loop fusion | flops 46079232 | bytes 92163072 | tf_op jit(solution)/shard_map/reduce_sum | solution.py:24
  132.9 39.3 %psum.7 = f32[768]{0:T(1024)S(1)} all-reduce(f32[768]{0:T(1024)S(1)} %fusion), channel_id=1, replica_groups=mesh['row'=4,'col'=8] {'row','col'}, use_global_device_ids=true, to_apply=%region_1.2 | all-reduce | flops 768 | bytes 6144 | tf_op jit(solution)/shard_map/psum | solution.py:25
  172.2 0.6 broadcast_multiply_fusion
where the time goes:
time: 173 us
  blocking collectives  64.5 us (37%)
  matrix products  44 us (25%)
  other arithmetic  40.3 us (23%)
  local copies, waits for them, and re-layouts  23.3 us (13%)
    dot_general x1, matrix products, shards(): jnp.einsum('abk,kp->abp', integrals, columns, preferred_element_type=jnp....  44 us
    psum x1, blocking collectives, shards(): pair_energy = lax.psum(partial_value, ('row', 'col')) / virtuals  39.3 us
    reduce_sum x1, other arithmetic, shards(): partial_value = jnp.sum(amplitudes.astype(jnp.float32) * full, axis=(0, 1))  39 us
    unnamed x1, local copies, waits for them, and re-layouts  22 us
    all_gather x1, blocking collectives, shards(): in_row = lax.all_gather(owned, 'col', axis=0, tiled=True)  15.6 us
    all_gather x1, blocking collectives, shards(): columns = lax.all_gather(in_row, 'row', axis=0, tiled=True)  9.5 us

commit v1 on v0

--- a/solution.py
+++ b/solution.py
@@ -1,7 +1,17 @@
+import functools
 import jax
 import jax.numpy as jnp
 from jax import lax
 from jax.sharding import PartitionSpec as P
+
+
+def hubs_feed(a0, dev_axis, axis_tag):
+    for i0 in (dev_axis, axis_tag):
+        a0 = jax.lax.psum(a0, i0)
+    return a0
+
+
+draw_teams = functools.partial(hubs_feed, dev_axis="col", axis_tag="row")
 
 
 def shards(amplitudes, integrals, window_index):
@@ -22,7 +32,7 @@
     columns = lax.all_gather(in_row, "row", axis=0, tiled=True)
     full = jnp.einsum("abk,kp->abp", integrals, columns, preferred_element_type=jnp.float32)
     partial_value = jnp.sum(amplitudes.astype(jnp.float32) * full, axis=(0, 1))
-    pair_energy = lax.psum(partial_value, ("row", "col")) / virtuals
+    pair_energy = draw_teams(partial_value) / virtuals
     residual = full.astype(jnp.bfloat16)
     return (residual, pair_energy)
 

time: 173 us -> 158 us (0.913)
  blocking collectives: 64.5 us -> 49 us
    psum x1 -> x2, blocking collectives: 39.3 us -> 23.9 us  [hubs_feed(): a0 = jax.lax.psum(a0, i0)]
where the time goes in v1:
time: 158 us; the launch traced here: 157 us
  blocking collectives  49 us (31%)
  matrix products  44 us (28%)
  other arithmetic  40.3 us (26%)
  local copies, waits for them, and re-layouts  23.3 us (15%)
    dot_general x1, matrix products, shards(): jnp.einsum('abk,kp->abp', integrals, columns, preferred_element_type=jnp....  44 us
    reduce_sum x1, other arithmetic, shards(): partial_value = jnp.sum(amplitudes.astype(jnp.float32) * full, axis=(0, 1))  39 us
    psum x2, blocking collectives, hubs_feed(): a0 = jax.lax.psum(a0, i0)  23.9 us
    unnamed x1, local copies, waits for them, and re-layouts  22 us
    all_gather x1, blocking collectives, shards(): in_row = lax.all_gather(owned, 'col', axis=0, tiled=True)  15.6 us
    all_gather x1, blocking collectives, shards(): columns = lax.all_gather(in_row, 'row', axis=0, tiled=True)  9.5 us

profile of v1, /device:TPU:0, one launch (start us, length us, event | category | flops | bytes accessed | tf_op | source)
XLA Modules:
  0.0 157.3 jit_solution(8882188267111788631)
XLA Ops:
  0.6 0.8 fusion.7
  1.4 1.4 gather_fusion
  2.8 15.6 %all_gather.6 = bf16[64,768]{1,0:T(8,128)(2,1)S(1)} all-gather(bf16[8,768]{1,0:T(8,128)(2,1)S(1)} %gather_fusion), channel_id=1, replica_groups=mesh['row'=4,'col'=8] {'col'}, dimensions={0}, use_global_device_ids=true | all-gather | bytes 110592 | tf_op jit(solution)/shard_map/all_gather | solution.py:31
  18.4 9.5 %all_gather.7 = bf16[256,768]{1,0:T(8,128)(2,1)S(1)} all-gather(bf16[64,768]{1,0:T(8,128)(2,1)S(1)} %all_gather.6), channel_id=1, replica_groups=mesh['row'=4,'col'=8] {'row'}, dimensions={0}, use_global_device_ids=true | all-gather | bytes 491520 | tf_op jit(solution)/shard_map/all_gather | solution.py:32
  27.9 44.0 %bitcast_convert_fusion = (bf16[200,100,768]{2,1,0:T(8,128)(2,1)}, f32[768,200,100]{0,2,1:T(8,128)}) fusion(bf16[200,100,256]{2,0,1:T(8,128)(2,1)} %param.4, bf16[256,768]{1,0:T(8,128)(2,1)S(1)} %all_gather.7), kind=kOutput, calls=%fused_computation.2 | convolution fusion | flops 7879680000 | bytes 102793216 | tf_op jit(solution)/shard_map/abk,kp->abp/dot_general | solution.py:33
  71.9 22.0 %copy.7 = bf16[200,100,768]{2,0,1:T(8,128)(2,1)} copy(bf16[200,100,768]{2,1,0:T(8,128)(2,1)} %get-tuple-element.4) | data formatting | bytes 61440000
  93.9 39.0 %fusion = f32[768]{0:T(1024)S(1)} fusion(f32[768,200,100]{0,2,1:T(8,128)} %get-tuple-element.5, bf16[200,100,768]{2,0,1:T(8,128)(2,1)} %param.3), kind=kLoop, calls=%fused_computation.3 | loop fusion | flops 46079232 | bytes 92163072 | tf_op jit(solution)/shard_map/reduce_sum | solution.py:34
  132.9 14.9 %psum.14 = f32[768]{0:T(1024)S(1)} all-reduce(f32[768]{0:T(1024)S(1)} %fusion), channel_id=1, replica_groups=mesh['row'=4,'col'=8] {'col'}, use_global_device_ids=true, to_apply=%region_1.2 | all-reduce | flops 768 | bytes 6144 | tf_op jit(solution)/shard_map/psum | solution.py:10
  147.8 9.0 %psum.15 = f32[768]{0:T(1024)S(1)} all-reduce(f32[768]{0:T(1024)S(1)} %psum.14), channel_id=1, replica_groups=mesh['row'=4,'col'=8] {'row'}, use_global_device_ids=true, to_apply=%region_2.3 | all-reduce | flops 768 | bytes 6144 | tf_op jit(solution)/shard_map/psum | solution.py:10
  156.7 0.6 broadcast_multiply_fusion

commit v2 on v0

--- a/solution.py
+++ b/solution.py
@@ -19,7 +19,10 @@
     col_offset = owned_index % virtuals - col_rank * block_cols
     owned = amplitudes[row_offset, col_offset]
     in_row = lax.all_gather(owned, "col", axis=0, tiled=True)
-    columns = lax.all_gather(in_row, "row", axis=0, tiled=True)
+    n_dev = lax.axis_size("row")
+    shards_2 = jnp.stack([in_row for _ in range(n_dev)])
+    shards_2 = lax.all_to_all(shards_2, "row", split_axis=0, concat_axis=0)
+    columns = jnp.concatenate(shards_2, axis=0)
     full = jnp.einsum("abk,kp->abp", integrals, columns, preferred_element_type=jnp.float32)
     partial_value = jnp.sum(amplitudes.astype(jnp.float32) * full, axis=(0, 1))
     pair_energy = lax.psum(partial_value, ("row", "col")) / virtuals

time: 173 us -> 175 us (1.012)
    all_to_all x0 -> x1, blocking collectives: none -> 11.1 us  [shards(): shards_2 = lax.all_to_all(shards_2, 'row', split_axis=0, concat_axis=0)]
    all_gather x1 -> x0, blocking collectives: 9.5 us -> none  [shards(): columns = lax.all_gather(in_row, 'row', axis=0, tiled=True)]
where the time goes in v2:
time: 175 us; the launch traced here: 174 us
  blocking collectives  66.1 us (38%)
  matrix products  44 us (25%)
  other arithmetic  40.3 us (23%)
  local copies, waits for them, and re-layouts  23.4 us (13%)
    dot_general x1, matrix products, shards(): jnp.einsum('abk,kp->abp', integrals, columns, preferred_element_type=jnp....  44 us
    psum x1, blocking collectives, shards(): pair_energy = lax.psum(partial_value, ('row', 'col')) / virtuals  39.3 us
    reduce_sum x1, other arithmetic, shards(): partial_value = jnp.sum(amplitudes.astype(jnp.float32) * full, axis=(0, 1))  39 us
    unnamed x1, local copies, waits for them, and re-layouts  22 us
    all_gather x1, blocking collectives, shards(): in_row = lax.all_gather(owned, 'col', axis=0, tiled=True)  15.6 us
    all_to_all x1, blocking collectives, shards(): shards_2 = lax.all_to_all(shards_2, 'row', split_axis=0, concat_axis=0)  11.1 us

profile of v2, /device:TPU:0, one launch (start us, length us, event | category | flops | bytes accessed | tf_op | source)
XLA Modules:
  0.0 174.4 jit_solution(2745551312663706725)
XLA Ops:
  0.6 0.8 fusion.6
  1.4 1.4 gather_fusion
  2.8 15.6 %all_gather.3 = bf16[64,768]{1,0:T(8,128)(2,1)S(1)} all-gather(bf16[8,768]{1,0:T(8,128)(2,1)S(1)} %gather_fusion), channel_id=1, replica_groups=mesh['row'=4,'col'=8] {'col'}, dimensions={0}, use_global_device_ids=true | all-gather | bytes 110592 | tf_op jit(solution)/shard_map/all_gather | solution.py:21
  18.4 11.1 %all_to_all.5 = bf16[4,64,768]{2,1,0:T(8,128)(2,1)S(1)} all-to-all(bf16[4,64,768]{2,1,0:T(8,128)(2,1)S(1)} %stack.2), channel_id=1, replica_groups=mesh['row'=4,'col'=8] {'row'}, dimensions={0} | all-to-all | bytes 786432 | tf_op jit(solution)/shard_map/all_to_all | solution.py:24
  29.6 44.0 %bitcast_convert_fusion = (bf16[200,100,768]{2,1,0:T(8,128)(2,1)}, f32[768,200,100]{0,2,1:T(8,128)}) fusion(bf16[256,768,1]{1,0,2:T(8,128)(2,1)S(1)} %bitcast.9, bf16[200,100,256]{2,0,1:T(8,128)(2,1)} %param.4), kind=kOutput, calls=%fused_computation.2 | convolution fusion | flops 7879680000 | bytes 102793216 | tf_op jit(solution)/shard_map/abk,kp->abp/dot_general | solution.py:26
  73.6 22.0 %copy.7 = bf16[200,100,768]{2,0,1:T(8,128)(2,1)} copy(bf16[200,100,768]{2,1,0:T(8,128)(2,1)} %get-tuple-element.4) | data formatting | bytes 61440000
  95.6 39.0 %fusion = f32[768]{0:T(1024)S(1)} fusion(f32[768,200,100]{0,2,1:T(8,128)} %get-tuple-element.5, bf16[200,100,768]{2,0,1:T(8,128)(2,1)} %param.3), kind=kLoop, calls=%fused_computation.3 | loop fusion | flops 46079232 | bytes 92163072 | tf_op jit(solution)/shard_map/reduce_sum | solution.py:27
  134.5 39.3 %psum.7 = f32[768]{0:T(1024)S(1)} all-reduce(f32[768]{0:T(1024)S(1)} %fusion), channel_id=1, replica_groups=mesh['row'=4,'col'=8] {'row','col'}, use_global_device_ids=true, to_apply=%region_1.2 | all-reduce | flops 768 | bytes 6144 | tf_op jit(solution)/shard_map/psum | solution.py:28
  173.8 0.6 broadcast_multiply_fusion
  (1 shorter events, 0.0 us)
